TPU v7x, 32 devices: a whole 2x2x4 slice. The times are simulated.
32 devices in a mesh: vtx: 8 (over z, x), src: 4 (over y, core).
Axes of the slice: x: 2, y: 2, z: 4, core: 2. Of those that a mesh axis runs over, the one named last changes fastest.
Arguments:
- heat: float32 [64, 64, 8192], P(None, ('vtx', 'src')), may hold values from -12 to 12
- cotan: float32 [4, 64, 8192], P(None, 'vtx'), may hold values from 0.2 to 2
- source_index: int32 [64], replicated, may hold values from 0 to 524287
Outputs:
- normalised: float32 [64, 64, 8192], P('src', 'vtx')
- col_norm: float32 [64], P('src')
Inputs may be any that keep to these rules, and one draw needn't show every extreme that they name: `source_index`: row-major vertex indices, sources may share a vertex.
All inputs are finite; a program needn't handle non-finite values.
Results may differ from a plain program's by a relative error of at most 0.0003.
Values sent between devices are 32-bit elements; how exact they have to be, the bound alone decides.
A program may use at most 64 MiB of HBM per device.

v0:
```python
import math
import jax
import jax.numpy as jnp
from jax import lax
from jax.sharding import PartitionSpec as P


def from_behind(value, axis, by):
    peers = lax.axis_size(axis)
    pairs = [(i, i + by) for i in range(peers) if 0 <= i + by < peers]
    return lax.ppermute(value, axis, pairs)


def extended(value, sides, width):
    for axis, dim in sides:
        peers, length = (lax.axis_size(axis), value.shape[dim])
        up = [(i, (i + 1) % peers) for i in range(peers - 1)]
        down = [(j, i) for i, j in up]
        last = lax.slice_in_dim(value, length - width, length, axis=dim)
        first = lax.slice_in_dim(value, 0, width, axis=dim)
        before = lax.ppermute(last, axis, up)
        after = lax.ppermute(first, axis, down)
        value = jnp.concatenate([before, value, after], axis=dim)
    return value


def from_right(values):
    return jnp.concatenate([values[..., 1:], jnp.zeros_like(values[..., :1])], axis=-1)


def from_left(values):
    return jnp.concatenate([jnp.zeros_like(values[..., :1]), values[..., :-1]], axis=-1)


def masked_cotan(cotan, row_start, total_rows):
    shape = cotan.shape[1:]
    rows = row_start + lax.broadcasted_iota(jnp.int32, shape, 0)
    cols = lax.broadcasted_iota(jnp.int32, shape, 1)
    inside_col = cols < shape[1] - 1
    inside_row = rows < total_rows - 1
    mass = cotan[0]
    east = jnp.where(inside_col, cotan[1], 0.0)
    north = jnp.where(inside_row, cotan[2], 0.0)
    diag = jnp.where(inside_col & inside_row, cotan[3], 0.0)
    return (mass, east, north, diag)


def stencil_defect(padded, mass, east, north_ext, diag_ext, row_start, sources, amplitude):
    center = padded[:, 1:-1, :]
    above = padded[:, 2:, :]
    below = padded[:, :-2, :]
    north = north_ext[1:]
    south_weight = north_ext[:-1]
    diag = diag_ext[1:]
    southwest_weight = from_left(diag_ext[:-1])
    west_weight = from_left(east)
    result = mass * center + east * (center - from_right(center))
    result = result + west_weight * (center - from_left(center))
    result = result + north * (center - above) + south_weight * (center - below)
    result = (
        result
        + diag * (center - from_right(above))
        + southwest_weight * (center - from_left(below))
    )
    count_rows, width = (center.shape[1], center.shape[2])
    row_ids = row_start + lax.broadcasted_iota(jnp.int32, (count_rows, width), 0)
    col_ids = lax.broadcasted_iota(jnp.int32, (count_rows, width), 1)
    flat = row_ids * width + col_ids
    delta = (flat[None, :, :] == sources[:, None, None]).astype(jnp.float32)
    return result - amplitude * delta


def on_device(heat, cotan, source_index):
    vtx_index = lax.axis_index("vtx")
    rows_dev = cotan.shape[1]
    width = cotan.shape[2]
    total_rows = rows_dev * lax.axis_size("vtx")
    amplitude = math.sqrt(total_rows * width) / 8.0
    block_start = vtx_index * rows_dev
    mass, east, north, diag = masked_cotan(cotan, block_start, total_rows)
    lower = from_behind(jnp.stack([north[-1:], diag[-1:]]), "vtx", 1)
    north_ext = jnp.concatenate([lower[0], north], axis=0)
    diag_ext = jnp.concatenate([lower[1], diag], axis=0)
    src_index = lax.axis_index("src")
    per_group = heat.shape[0] // lax.axis_size("src")
    tile = lax.all_to_all(heat, "src", split_axis=0, concat_axis=1, tiled=True)
    padded = extended(tile, (("vtx", 1),), 1)
    sources = lax.dynamic_slice_in_dim(source_index, src_index * per_group, per_group)
    defect = stencil_defect(
        padded, mass, east, north_ext, diag_ext, block_start, sources, amplitude
    )
    total = lax.psum(jnp.sum(defect * defect, axis=(1, 2)), "vtx")
    norms = jnp.sqrt(total / (total_rows * width) + 1e-06)
    return (defect / norms[:, None, None], norms)


def solution(mesh):
    return jax.shard_map(
        on_device,
        mesh=mesh,
        in_specs=(P(None, ("vtx", "src"), None), P(None, "vtx", None), P()),
        out_specs=(P("src", "vtx", None), P("src")),
        check_vma=False,
    )
```

profile of v0, /device:TPU:0, one launch (start us, length us, event | category | flops | bytes accessed | tf_op | source)
XLA Modules:
  0.0 121.2 jit_solution(14948934049001628183)
XLA Ops:
  0.6 0.0 copy-start
  0.6 5.0 %all-to-all-start = ((f32[64,2,8192]{2,1,0:T(2,128)}), f32[64,2,8192]{2,1,0:T(2,128)}, u32[]{:S(2)}, u32[]{:S(2)}) async-start(f32[64,2,8192]{2,1,0:T(2,128)} %param.3), calls=%async_computation | async-start | bytes 8388608 | tf_op jit(solution)/shard_map/all_to_all | solution.py:86
  5.6 0.0 copy-start.2
  5.7 0.0 copy-done
  5.7 0.1 bitcast_select_fusion.1
  5.9 0.1 pad_maximum_fusion.1
  5.9 4.9 %collective-permute-start.1 = (f32[2,1,8192]{2,1,0:T(1,128)S(1)}, f32[2,1,8192]{2,1,0:T(1,128)S(1)}, u32[]{:S(2)}, u32[]{:S(2)}) collective-permute-start(f32[2,1,8192]{2,1,0:T(1,128)S(1)} %pad_maximum_fusion.1), channel_id=1, source_target_pairs={{0,4},{4,8},{8,12},{12,16},{16,20},{20,24},{24,28},{1,5},{5,9},{9,... | collective-permute-start | bytes 196616 | tf_op jit(solution)/shard_map/ppermute | solution.py:11
  10.8 0.1 slice_bitcast_fusion
  11.0 0.1 iota_add_fusion
  11.1 0.0 copy-done.2
  11.1 0.1 dynamic_slice.3
  11.2 0.1 concatenate.32
  11.3 1.4 %collective-permute-done.1 = f32[2,1,8192]{2,1,0:T(1,128)S(1)} collective-permute-done((f32[2,1,8192]{2,1,0:T(1,128)S(1)}, f32[2,1,8192]{2,1,0:T(1,128)S(1)}, u32[]{:S(2)}, u32[]{:S(2)}) %collective-permute-start.1) | collective-permute-done | bytes 65568 | tf_op jit(solution)/shard_map/ppermute | solution.py:11
  12.8 0.2 select_maximum_fusion.2
  13.0 41.6 %all-to-all-done = f32[64,2,8192]{2,1,0:T(2,128)} async-done(((f32[64,2,8192]{2,1,0:T(2,128)}), f32[64,2,8192]{2,1,0:T(2,128)}, u32[]{:S(2)}, u32[]{:S(2)}) %all-to-all-start) | async-done | bytes 4194336 | tf_op jit(solution)/shard_map/all_to_all | solution.py:86
  54.5 4.6 %copy.6 = f32[4,16,2,8192]{3,1,2,0:T(8,128)S(1)} copy(f32[4,16,2,8192]{3,2,1,0:T(2,128)} %bitcast.1) | data formatting | bytes 8388608 | tf_op jit(solution)/shard_map/all_to_all | solution.py:86
  59.2 0.1 fusion.19
  59.2 1.3 %collective-permute-start = (f32[16,1,8192]{2,0,1:T(8,128)S(1)}, f32[16,1,8192]{2,0,1:T(8,128)S(1)}, u32[]{:S(2)}, u32[]{:S(2)}) collective-permute-start(f32[16,1,8192]{2,0,1:T(8,128)S(1)} %get-tuple-element.8), channel_id=1, source_target_pairs={{4,0},{8,4},{12,8},{16,12},{20,16},{24,20},{28,24},{5,1},{9,5},{13... | collective-permute-start | bytes 1572872 | tf_op jit(solution)/shard_map/ppermute | solution.py:22
  60.5 4.8 %collective-permute-start.2 = (f32[16,1,8192]{2,0,1:T(8,128)S(1)}, f32[16,1,8192]{2,0,1:T(8,128)S(1)}, u32[]{:S(2)}, u32[]{:S(2)}) collective-permute-start(f32[16,1,8192]{2,0,1:T(8,128)S(1)} %get-tuple-element.9), channel_id=1, source_target_pairs={{0,4},{4,8},{8,12},{12,16},{16,20},{20,24},{24,28},{1,5},{5,9},{9,... | collective-permute-start | bytes 1572872 | tf_op jit(solution)/shard_map/ppermute | solution.py:21
  65.4 1.5 %fusion.18 = (f32[16,8,8191]{2,0,1:T(8,128)S(1)}, f32[16,8,8191]{2,0,1:T(8,128)S(1)}) fusion(f32[16,8,8192]{2,0,1:T(8,128)S(1)} %bitcast.28), kind=kLoop, calls=%fused_computation.47 | loop fusion | bytes 16775168 | tf_op jit(solution)/shard_map/slice | solution.py:28
  66.8 8.2 %collective-permute-done = f32[16,1,8192]{2,0,1:T(8,128)S(1)} collective-permute-done((f32[16,1,8192]{2,0,1:T(8,128)S(1)}, f32[16,1,8192]{2,0,1:T(8,128)S(1)}, u32[]{:S(2)}, u32[]{:S(2)}) %collective-permute-start) | collective-permute-done | bytes 524320 | tf_op jit(solution)/shard_map/ppermute | solution.py:22
  75.0 11.4 %collective-permute-done.2 = f32[16,1,8192]{2,0,1:T(8,128)S(1)} collective-permute-done((f32[16,1,8192]{2,0,1:T(8,128)S(1)}, f32[16,1,8192]{2,0,1:T(8,128)S(1)}, u32[]{:S(2)}, u32[]{:S(2)}) %collective-permute-start.2) | collective-permute-done | bytes 524320 | tf_op jit(solution)/shard_map/ppermute | solution.py:21
  86.4 7.7 %multiply_reduce_fusion = (f32[16]{0:T(128)S(1)}, f32[16,8,8192]{2,0,1:T(8,128)}) fusion(s32[16]{0:T(128)S(1)} %dynamic_slice.3, s32[8,8192]{1,0:T(8,128)S(1)} %iota_add_fusion, f32[16,8,8192]{2,0,1:T(8,128)S(1)} %bitcast.29, f32[16,1,8192]{2,0,1:T(8,128)S(1)} %collective-permute-done.2, f32[8,8192]{1,0:T(8,128)S(1)} %get-tuple-element.22, ...), kind=kLoop, calls=%fused_computation.23 | loop fusion | flops 35651568 | bytes 19922048 | tf_op jit(solution)/shard_map/reduce_sum | solution.py:92
  94.1 19.8 %psum.7 = f32[16]{0:T(128)S(1)} all-reduce(f32[16]{0:T(128)S(1)} %get-tuple-element.4), channel_id=1, replica_groups=mesh['vtx'=8,'src'=4] {'vtx'}, use_global_device_ids=true, to_apply=%region_1.2 | all-reduce | flops 16 | bytes 128 | tf_op jit(solution)/shard_map/psum | solution.py:92
  114.0 0.0 copy-start.1
  114.0 2.7 %broadcast_divide_fusion = f32[16,8,8192]{2,0,1:T(8,128)S(1)} fusion(f32[16,8,8192]{2,0,1:T(8,128)} %get-tuple-element.5, f32[16]{0:T(128)S(1)} %add_sqrt_fusion), kind=kLoop, calls=%fused_computation.24 | loop fusion | flops 1048576 | bytes 8388672 | tf_op jit(solution)/shard_map/div | solution.py:94
  116.7 0.0 copy-done.1
  116.7 4.4 %copy.7 = f32[16,8,8192]{2,1,0:T(8,128)} copy(f32[16,8,8192]{2,0,1:T(8,128)S(1)} %broadcast_divide_fusion) | data formatting | bytes 8388608
  (8 shorter events, 0.1 us)
Async XLA Ops:
  0.6 5.0 %copy-start = (f32[4,8,8192]{2,1,0:T(8,128)S(1)}, f32[4,8,8192]{2,1,0:T(8,128)}, u32[]{:S(2)}) copy-start(f32[4,8,8192]{2,1,0:T(8,128)} %param.4) | copy-start | bytes 3145732
  0.6 53.9 %all-to-all-start = ((f32[64,2,8192]{2,1,0:T(2,128)}), f32[64,2,8192]{2,1,0:T(2,128)}, u32[]{:S(2)}, u32[]{:S(2)}) async-start(f32[64,2,8192]{2,1,0:T(2,128)} %param.3), calls=%async_computation | async-start | bytes 8388608 | tf_op jit(solution)/shard_map/all_to_all | solution.py:86
  5.6 5.5 %copy-start.2 = (s32[64]{0:T(128)S(1)}, s32[64]{0:T(128)}, u32[]{:S(2)}) copy-start(s32[64]{0:T(128)} %param.5) | copy-start | bytes 772
  5.9 6.8 %collective-permute-start.1 = (f32[2,1,8192]{2,1,0:T(1,128)S(1)}, f32[2,1,8192]{2,1,0:T(1,128)S(1)}, u32[]{:S(2)}, u32[]{:S(2)}) collective-permute-start(f32[2,1,8192]{2,1,0:T(1,128)S(1)} %pad_maximum_fusion.1), channel_id=1, source_target_pairs={{0,4},{4,8},{8,12},{12,16},{16,20},{20,24},{24,28},{1,5},{5,9},{9,... | collective-permute-start | bytes 196616 | tf_op jit(solution)/shard_map/ppermute | solution.py:11
  59.2 15.8 %collective-permute-start = (f32[16,1,8192]{2,0,1:T(8,128)S(1)}, f32[16,1,8192]{2,0,1:T(8,128)S(1)}, u32[]{:S(2)}, u32[]{:S(2)}) collective-permute-start(f32[16,1,8192]{2,0,1:T(8,128)S(1)} %get-tuple-element.8), channel_id=1, source_target_pairs={{4,0},{8,4},{12,8},{16,12},{20,16},{24,20},{28,24},{5,1},{9,5},{13... | collective-permute-start | bytes 1572872 | tf_op jit(solution)/shard_map/ppermute | solution.py:22
  60.5 25.9 %collective-permute-start.2 = (f32[16,1,8192]{2,0,1:T(8,128)S(1)}, f32[16,1,8192]{2,0,1:T(8,128)S(1)}, u32[]{:S(2)}, u32[]{:S(2)}) collective-permute-start(f32[16,1,8192]{2,0,1:T(8,128)S(1)} %get-tuple-element.9), channel_id=1, source_target_pairs={{0,4},{4,8},{8,12},{12,16},{16,20},{20,24},{24,28},{1,5},{5,9},{9,... | collective-permute-start | bytes 1572872 | tf_op jit(solution)/shard_map/ppermute | solution.py:21
  114.0 2.7 %copy-start.1 = (f32[16]{0:T(128)}, f32[16]{0:T(128)S(1)}, u32[]{:S(2)}) copy-start(f32[16]{0:T(128)S(1)} %add_sqrt_fusion) | copy-start | bytes 196
where the time goes:
time: 122 us; the launch traced here: 121 us
  waiting for transfers between devices  62.6 us (51%)
  blocking collectives  19.8 us (16%)
  starting transfers between devices  15.9 us (13%)
  other arithmetic  11.1 us (9%)
  local copies, waits for them, and re-layouts  10.9 us (9%)
    all_to_all x1, waiting for transfers between devices, on_device(): tile = lax.all_to_all(heat, 'src', split_axis=0, concat_axis=1, tiled=True)  41.6 us
    psum x1, blocking collectives, on_device(): total = lax.psum(jnp.sum(defect * defect, axis=(1, 2)), 'vtx')  19.8 us
    ppermute x1, waiting for transfers between devices, extended(): before = lax.ppermute(last, axis, up)  11.4 us
    ppermute x1, waiting for transfers between devices, extended(): after = lax.ppermute(first, axis, down)  8.19 us
    reduce_sum x1, other arithmetic, on_device(): total = lax.psum(jnp.sum(defect * defect, axis=(1, 2)), 'vtx')  7.71 us
    all_to_all x1, starting transfers between devices, on_device(): tile = lax.all_to_all(heat, 'src', split_axis=0, concat_axis=1, tiled=True)  4.97 us
    ppermute x1, starting transfers between devices, from_behind(): return lax.ppermute(value, axis, pairs)  4.87 us
    ppermute x1, starting transfers between devices, extended(): before = lax.ppermute(last, axis, up)  4.81 us
  transfers between devices with their start and end apart: 4, of which 4 were waited for; matrix products, arithmetic and copies ran while one was open for 2% of the time, Pallas kernels for 0%

commit v1 on v0

--- a/solution.py
+++ b/solution.py
@@ -89,7 +89,9 @@
     defect = stencil_defect(
         padded, mass, east, north_ext, diag_ext, block_start, sources, amplitude
     )
-    total = lax.psum(jnp.sum(defect * defect, axis=(1, 2)), "vtx")
+    own = jnp.sum(defect * defect, axis=(1, 2))
+    parts = lax.all_gather(own, "vtx", axis=0, tiled=False)
+    total = parts.sum(axis=0)
     norms = jnp.sqrt(total / (total_rows * width) + 1e-06)
     return (defect / norms[:, None, None], norms)
 

time: 122 us -> 127 us (1.041)
  waiting for transfers between devices: 62.6 us -> 65.3 us
    psum x1 -> x0, blocking collectives: 19.8 us -> none  [on_device(): total = lax.psum(jnp.sum(defect * defect, axis=(1, 2)), 'vtx')]
    unnamed x0 -> x1, blocking collectives: none -> 19.8 us
    all_to_all x1, waiting for transfers between devices: 41.6 us -> 46.2 us  [on_device(): tile = lax.all_to_all(heat, 'src', split_axis=0, concat_axis=1, tiled=True)]
    ppermute x1, waiting for transfers between devices: 1.44 us -> 0.01 us  [from_behind(): return lax.ppermute(value, axis, pairs)]
    unnamed x7 -> x12, local copies, waits for them, and re-layouts: 4.46 us -> 5.29 us
    reduce_sum x1 -> x2, other arithmetic: 7.71 us -> 7.73 us  [the longest x1 7.71 us: on_device(): own = jnp.sum(defect * defect, axis=(1, 2))]
  transfers between devices with their start and end apart: 4 -> 4, of which waited for: 4 -> 3; matrix products, arithmetic and copies ran while one was open for 2% -> 2% of each run, Pallas kernels for 0% -> 0%
where the time goes in v1:
time: 127 us; the launch traced here: 126 us
  waiting for transfers between devices  65.3 us (51%)
  blocking collectives  19.8 us (16%)
  starting transfers between devices  15.7 us (12%)
  other arithmetic  12.1 us (10%)
  local copies, waits for them, and re-layouts  11.8 us (9%)
  between operations  1.51 us (1%)
    all_to_all x1, waiting for transfers between devices, on_device(): tile = lax.all_to_all(heat, 'src', split_axis=0, concat_axis=1, tiled=True)  46.2 us
    unnamed x1, blocking collectives  19.8 us
    ppermute x1, waiting for transfers between devices, extended(): before = lax.ppermute(last, axis, up)  11.2 us
    ppermute x1, waiting for transfers between devices, extended(): after = lax.ppermute(first, axis, down)  7.91 us
    reduce_sum x1, other arithmetic, on_device(): own = jnp.sum(defect * defect, axis=(1, 2))  7.71 us
    unnamed x12, local copies, waits for them, and re-layouts  5.29 us
    ppermute x1, starting transfers between devices, from_behind(): return lax.ppermute(value, axis, pairs)  5.01 us
    all_to_all x1, starting transfers between devices, on_device(): tile = lax.all_to_all(heat, 'src', split_axis=0, concat_axis=1, tiled=True)  4.85 us
  transfers between devices with their start and end apart: 4, of which 3 were waited for; matrix products, arithmetic and copies ran while one was open for 2% of the time, Pallas kernels for 0%

profile of v1, /device:TPU:0, one launch (start us, length us, event | category | flops | bytes accessed | tf_op | source)
XLA Modules:
  0.0 126.3 jit_solution(1844966854184624672)
XLA Ops:
  0.7 1.1 bitcast_select_fusion.1
  1.9 0.1 pad_maximum_fusion.1
  2.0 0.0 copy-start
  2.0 0.0 copy-start.2
  2.0 0.0 copy-start.3
  2.0 5.0 %collective-permute-start.1 = (f32[2,1,8192]{2,1,0:T(1,128)S(1)}, f32[2,1,8192]{2,1,0:T(1,128)S(1)}, u32[]{:S(2)}, u32[]{:S(2)}) collective-permute-start(f32[2,1,8192]{2,1,0:T(1,128)S(1)} %pad_maximum_fusion.1), channel_id=1, source_target_pairs={{0,4},{4,8},{8,12},{12,16},{16,20},{20,24},{24,28},{1,5},{5,9},{9,... | collective-permute-start | bytes 196616 | tf_op jit(solution)/shard_map/ppermute | solution.py:11
  7.0 4.8 %all-to-all-start = ((f32[64,2,8192]{2,1,0:T(2,128)}), f32[64,2,8192]{2,1,0:T(2,128)}, u32[]{:S(2)}, u32[]{:S(2)}) async-start(f32[64,2,8192]{2,1,0:T(2,128)} %param.3), calls=%async_computation | async-start | bytes 8388608 | tf_op jit(solution)/shard_map/all_to_all | solution.py:86
  11.9 0.0 copy-done
  11.9 0.1 slice_bitcast_fusion
  12.1 0.1 iota_add_fusion
  12.2 0.1 concatenate.32
  12.3 0.0 copy-done.2
  12.3 0.1 dynamic_slice.3
  12.4 0.0 copy-done.3
  12.4 0.6 dynamic-slice
  13.6 0.0 collective-permute-done.1
  13.6 0.2 select_maximum_fusion.2
  13.9 46.2 %all-to-all-done = f32[64,2,8192]{2,1,0:T(2,128)} async-done(((f32[64,2,8192]{2,1,0:T(2,128)}), f32[64,2,8192]{2,1,0:T(2,128)}, u32[]{:S(2)}, u32[]{:S(2)}) %all-to-all-start) | async-done | bytes 4194336 | tf_op jit(solution)/shard_map/all_to_all | solution.py:86
  60.1 4.6 %copy.6 = f32[4,16,2,8192]{3,1,2,0:T(8,128)S(1)} copy(f32[4,16,2,8192]{3,2,1,0:T(2,128)} %bitcast.1) | data formatting | bytes 8388608 | tf_op jit(solution)/shard_map/all_to_all | solution.py:86
  64.7 0.1 fusion.19
  64.8 1.3 %collective-permute-start = (f32[16,1,8192]{2,0,1:T(8,128)S(1)}, f32[16,1,8192]{2,0,1:T(8,128)S(1)}, u32[]{:S(2)}, u32[]{:S(2)}) collective-permute-start(f32[16,1,8192]{2,0,1:T(8,128)S(1)} %get-tuple-element.8), channel_id=1, source_target_pairs={{4,0},{8,4},{12,8},{16,12},{20,16},{24,20},{28,24},{5,1},{9,5},{13... | collective-permute-start | bytes 1572872 | tf_op jit(solution)/shard_map/ppermute | solution.py:22
  66.1 4.6 %collective-permute-start.2 = (f32[16,1,8192]{2,0,1:T(8,128)S(1)}, f32[16,1,8192]{2,0,1:T(8,128)S(1)}, u32[]{:S(2)}, u32[]{:S(2)}) collective-permute-start(f32[16,1,8192]{2,0,1:T(8,128)S(1)} %get-tuple-element.9), channel_id=1, source_target_pairs={{0,4},{4,8},{8,12},{12,16},{16,20},{20,24},{24,28},{1,5},{5,9},{9,... | collective-permute-start | bytes 1572872 | tf_op jit(solution)/shard_map/ppermute | solution.py:21
  70.7 1.5 %fusion.18 = (f32[16,8,8191]{2,0,1:T(8,128)S(1)}, f32[16,8,8191]{2,0,1:T(8,128)S(1)}) fusion(f32[16,8,8192]{2,0,1:T(8,128)S(1)} %bitcast.29), kind=kLoop, calls=%fused_computation.47 | loop fusion | bytes 16775168 | tf_op jit(solution)/shard_map/slice | solution.py:28
  72.1 7.9 %collective-permute-done = f32[16,1,8192]{2,0,1:T(8,128)S(1)} collective-permute-done((f32[16,1,8192]{2,0,1:T(8,128)S(1)}, f32[16,1,8192]{2,0,1:T(8,128)S(1)}, u32[]{:S(2)}, u32[]{:S(2)}) %collective-permute-start) | collective-permute-done | bytes 524320 | tf_op jit(solution)/shard_map/ppermute | solution.py:22
  80.0 11.2 %collective-permute-done.2 = f32[16,1,8192]{2,0,1:T(8,128)S(1)} collective-permute-done((f32[16,1,8192]{2,0,1:T(8,128)S(1)}, f32[16,1,8192]{2,0,1:T(8,128)S(1)}, u32[]{:S(2)}, u32[]{:S(2)}) %collective-permute-start.2) | collective-permute-done | bytes 524320 | tf_op jit(solution)/shard_map/ppermute | solution.py:21
  91.2 7.7 %multiply_reduce_fusion = (f32[16]{0:T(128)S(1)}, f32[16,8,8192]{2,0,1:T(8,128)}) fusion(s32[16]{0:T(128)S(1)} %dynamic_slice.3, s32[8,8192]{1,0:T(8,128)S(1)} %iota_add_fusion, f32[16,8,8192]{2,0,1:T(8,128)S(1)} %bitcast.30, f32[16,1,8192]{2,0,1:T(8,128)S(1)} %collective-permute-done.2, f32[8,8192]{1,0:T(8,128)S(1)} %get-tuple-element.22, ...), kind=kLoop, calls=%fused_computation.23 | loop fusion | flops 35651568 | bytes 19922048 | tf_op jit(solution)/shard_map/reduce_sum | solution.py:92
  98.9 0.2 dynamic-update-slice
  99.2 19.8 %all-reduce.6 = f32[128]{0:T(128)S(1)} all-reduce(f32[128]{0:T(128)S(1)} %dynamic-update-slice), channel_id=2, replica_groups=mesh['vtx'=8,'src'=4] {'vtx'}, use_global_device_ids=true, to_apply=%add.6 | all-reduce | flops 128 | bytes 1024
  119.0 0.1 reshape.77
  119.1 0.0 copy-start.1
  119.1 2.7 %broadcast_divide_fusion = f32[16,8,8192]{2,0,1:T(8,128)S(1)} fusion(f32[16,8,8192]{2,0,1:T(8,128)} %get-tuple-element.5, f32[16]{0:T(128)S(1)} %add_sqrt_fusion), kind=kLoop, calls=%fused_computation.24 | loop fusion | flops 1048576 | bytes 8388672 | tf_op jit(solution)/shard_map/div | solution.py:96
  121.9 0.0 copy-done.1
  121.9 4.4 %copy.7 = f32[16,8,8192]{2,1,0:T(8,128)} copy(f32[16,8,8192]{2,0,1:T(8,128)S(1)} %broadcast_divide_fusion) | data formatting | bytes 8388608
  (10 shorter events, 0.2 us)
Async XLA Ops:
  2.0 9.9 %copy-start = (f32[4,8,8192]{2,1,0:T(8,128)S(1)}, f32[4,8,8192]{2,1,0:T(8,128)}, u32[]{:S(2)}) copy-start(f32[4,8,8192]{2,1,0:T(8,128)} %param.4) | copy-start | bytes 3145732
  2.0 10.3 %copy-start.2 = (s32[64]{0:T(128)S(1)}, s32[64]{0:T(128)}, u32[]{:S(2)}) copy-start(s32[64]{0:T(128)} %param.5) | copy-start | bytes 772
  2.0 10.4 %copy-start.3 = (u32[32]{0:T(128)S(1)}, u32[32]{0:T(128)}, u32[]{:S(2)}) copy-start(u32[32]{0:T(128)} %constant.50) | copy-start | bytes 388
  2.0 11.6 %collective-permute-start.1 = (f32[2,1,8192]{2,1,0:T(1,128)S(1)}, f32[2,1,8192]{2,1,0:T(1,128)S(1)}, u32[]{:S(2)}, u32[]{:S(2)}) collective-permute-start(f32[2,1,8192]{2,1,0:T(1,128)S(1)} %pad_maximum_fusion.1), channel_id=1, source_target_pairs={{0,4},{4,8},{8,12},{12,16},{16,20},{20,24},{24,28},{1,5},{5,9},{9,... | collective-permute-start | bytes 196616 | tf_op jit(solution)/shard_map/ppermute | solution.py:11
  7.0 53.1 %all-to-all-start = ((f32[64,2,8192]{2,1,0:T(2,128)}), f32[64,2,8192]{2,1,0:T(2,128)}, u32[]{:S(2)}, u32[]{:S(2)}) async-start(f32[64,2,8192]{2,1,0:T(2,128)} %param.3), calls=%async_computation | async-start | bytes 8388608 | tf_op jit(solution)/shard_map/all_to_all | solution.py:86
  64.8 15.3 %collective-permute-start = (f32[16,1,8192]{2,0,1:T(8,128)S(1)}, f32[16,1,8192]{2,0,1:T(8,128)S(1)}, u32[]{:S(2)}, u32[]{:S(2)}) collective-permute-start(f32[16,1,8192]{2,0,1:T(8,128)S(1)} %get-tuple-element.8), channel_id=1, source_target_pairs={{4,0},{8,4},{12,8},{16,12},{20,16},{24,20},{28,24},{5,1},{9,5},{13... | collective-permute-start | bytes 1572872 | tf_op jit(solution)/shard_map/ppermute | solution.py:22
  66.1 25.2 %collective-permute-start.2 = (f32[16,1,8192]{2,0,1:T(8,128)S(1)}, f32[16,1,8192]{2,0,1:T(8,128)S(1)}, u32[]{:S(2)}, u32[]{:S(2)}) collective-permute-start(f32[16,1,8192]{2,0,1:T(8,128)S(1)} %get-tuple-element.9), channel_id=1, source_target_pairs={{0,4},{4,8},{8,12},{12,16},{16,20},{20,24},{24,28},{1,5},{5,9},{9,... | collective-permute-start | bytes 1572872 | tf_op jit(solution)/shard_map/ppermute | solution.py:21
  119.1 2.7 %copy-start.1 = (f32[16]{0:T(128)}, f32[16]{0:T(128)S(1)}, u32[]{:S(2)}) copy-start(f32[16]{0:T(128)S(1)} %add_sqrt_fusion) | copy-start | bytes 196
